TPU v7x, 32 devices: a whole 2x2x4 slice. The times are simulated.
32 devices in a mesh: dp: 4 (over z), table: 8 (over y, x, core).
Axes of the slice: x: 2, y: 2, z: 4, core: 2. Of those that a mesh axis runs over, the one named last changes fastest.
Arguments:
- table: bfloat16 [4096, 256], P('table'), may hold values from -6 to 6
- weights: bfloat16 [2, 6, 256, 256], replicated, may hold values from -0.375 to 0.375
- fetch_rows: int32 [4, 8, 8, 32], P('dp', 'table'), may hold values from 0 to 511
- fetch_count: int32 [4, 8, 8], P('dp', 'table'), may hold values from 1 to 32, as said below
- first_self: int32 [4, 8, 256], P('dp', 'table'), may hold values from 0 to 255, as said below
- first_edges: int32 [4, 8, 5, 256, 4], P('dp', 'table'), may hold values from 0 to 255, as said below
- first_degree: int32 [4, 8, 5, 256], P('dp', 'table'), may hold values from 1 to 4
- second_self: int32 [4, 8, 128], P('dp', 'table'), may hold values from 0 to 255
- second_edges: int32 [4, 8, 5, 128, 4], P('dp', 'table'), may hold values from 0 to 255
- second_degree: int32 [4, 8, 5, 128], P('dp', 'table'), may hold values from 1 to 4
- cotangent: bfloat16 [4, 8, 128, 256], P('dp', 'table'), may hold values from -6 to 6
Outputs:
- node_out: bfloat16 [4, 8, 128, 256], P('dp', 'table')
- weight_grad: bfloat16 [2, 6, 256, 256], replicated
- table_grad: float32 [8, 512, 256], P('table', 'dp')
Inputs may be any that keep to these rules, and one draw needn't show every extreme that they name: Minibatch (i, j) uses the first fetch_count[i, j, k] slots for shard k; for each i one shard is given all 32 slots by every minibatch of that i, and every other count is at most 16. `fetch_rows`: slots past the count hold arbitrary row numbers. `first_self`: every entry is a live slot k * 32 + c with c < fetch_count of shard k. `first_edges`: every entry, used or not, is a live slot k * 32 + c with c < fetch_count of shard k.
All inputs are finite; a program needn't handle non-finite values.
Results may differ from a plain program's by a relative error of at most 0.0057.
Values may be sent and summed in bfloat16 or wider, within the bound.
A program may use at most 64 MiB of HBM per device.

v0:
```python
import jax
import jax.numpy as jnp
from jax import lax
from jax.sharding import PartitionSpec as P


def aggregate(features, edges, degrees):

    def aggregate_single(bundle):
        indices, degree = bundle
        within = lax.broadcasted_iota(jnp.int32, indices.shape, 1) < degree[:, None]
        picked = jnp.where(within[:, :, None], features[indices], jnp.zeros((), features.dtype))
        summed = jnp.sum(picked.astype(jnp.float32), axis=1)
        return (summed / degree[:, None].astype(jnp.float32)).astype(jnp.bfloat16)

    return lax.map(aggregate_single, (edges, degrees))


def spread_back(grads, edges, degrees, height):

    def spread_single(running, bundle):
        part_grad, indices, degree = bundle
        within = lax.broadcasted_iota(jnp.int32, indices.shape, 1) < degree[:, None]
        scaled = part_grad / degree[:, None].astype(part_grad.dtype)
        placed = jnp.where(within[:, :, None], scaled[:, None, :], jnp.zeros((), part_grad.dtype))
        return (running.at[indices.reshape(-1)].add(placed.reshape(-1, part_grad.shape[-1])), None)

    initial = jnp.zeros((height, grads.shape[-1]), grads.dtype)
    result, ignored = lax.scan(spread_single, initial, (grads, edges, degrees))
    return result


def relation_sum(agg, layer_weights):
    return jnp.einsum("rbd,rde->be", agg, layer_weights, preferred_element_type=jnp.float32)


def silu_slope(preact):
    logistic = jax.nn.sigmoid(preact)
    return logistic * (1.0 + preact * (1.0 - logistic))


def weight_terms(own_rows, agg, grad):
    own_term = lax.dot_general(
        own_rows, grad, (((0,), (0,)), ((), ())), preferred_element_type=jnp.float32
    )
    rel_terms = jnp.einsum("rbd,be->rde", agg, grad, preferred_element_type=jnp.float32)
    return jnp.concatenate([own_term[None], rel_terms], axis=0)


def input_terms(grad, layer_weights):
    own_back = lax.dot_general(
        grad, layer_weights[0], (((1,), (1,)), ((), ())), preferred_element_type=jnp.float32
    )
    rel_back = jnp.einsum(
        "be,rde->rbd", grad, layer_weights[1:], preferred_element_type=jnp.float32
    )
    return (own_back, rel_back)


def body(
    table,
    weights,
    fetch_rows,
    fetch_count,
    first_self,
    first_edges,
    first_degree,
    second_self,
    second_edges,
    second_degree,
    cotangent,
):
    wanted = fetch_rows[0, 0]
    live_count = fetch_count[0, 0]
    first_self = first_self[0, 0]
    first_edges = first_edges[0, 0]
    first_degree = first_degree[0, 0]
    second_self = second_self[0, 0]
    second_edges = second_edges[0, 0]
    second_degree = second_degree[0, 0]
    cot_rows = cotangent[0, 0]
    shards = wanted.shape[0]
    width = wanted.shape[1]
    feature = table.shape[1]
    asked = lax.all_to_all(wanted, "table", split_axis=0, concat_axis=0, tiled=True)
    found = table[asked]
    fetched, asked = (
        lax.all_to_all(found, "table", split_axis=0, concat_axis=0, tiled=True),
        asked,
    )
    living = lax.broadcasted_iota(jnp.int32, wanted.shape, 1) < live_count[:, None]
    inputs = jnp.where(living[:, :, None], fetched, jnp.zeros((), fetched.dtype)).reshape(
        -1, feature
    )
    first_agg = aggregate(inputs, first_edges, first_degree)
    first_own = inputs[first_self]
    first_pre = jnp.dot(
        first_own, weights[0, 0], preferred_element_type=jnp.float32
    ) + relation_sum(first_agg, weights[0, 1:])
    hidden = jax.nn.silu(first_pre).astype(jnp.bfloat16)
    second_agg = aggregate(hidden, second_edges, second_degree)
    second_own = hidden[second_self]
    output = jnp.dot(second_own, weights[1, 0], preferred_element_type=jnp.float32) + relation_sum(
        second_agg, weights[1, 1:]
    )
    node_out = output.astype(jnp.bfloat16)
    grad_top = weight_terms(second_own, second_agg, cot_rows)
    own_back, rel_back = input_terms(cot_rows, weights[1])
    grad_hidden = (
        jnp.zeros((hidden.shape[0], hidden.shape[1]), jnp.float32).at[second_self].add(own_back)
    )
    grad_hidden = grad_hidden + spread_back(rel_back, second_edges, second_degree, hidden.shape[0])
    grad_pre = (grad_hidden * silu_slope(first_pre)).astype(jnp.bfloat16)
    grad_bottom = weight_terms(first_own, first_agg, grad_pre)
    own_back, rel_back = input_terms(grad_pre, weights[0])
    grad_slots = (
        jnp.zeros((inputs.shape[0], inputs.shape[1]), jnp.float32).at[first_self].add(own_back)
    )
    grad_slots = grad_slots + spread_back(rel_back, first_edges, first_degree, inputs.shape[0])
    grad_slots = jnp.where(living.reshape(-1)[:, None], grad_slots, jnp.zeros((), grad_slots.dtype))
    grad_bottom, grad_top = lax.psum((grad_bottom, grad_top), ("dp", "table"))
    seeds = cot_rows.shape[0] * lax.axis_size("dp") * lax.axis_size("table")
    weight_grad = (jnp.stack([grad_bottom, grad_top]) / jnp.sqrt(jnp.float32(seeds))).astype(
        jnp.bfloat16
    )
    slot_grads = grad_slots.reshape(shards, width, feature)
    returned = lax.all_to_all(slot_grads, "table", split_axis=0, concat_axis=0, tiled=True)
    dense = (
        jnp.zeros((table.shape[0], feature), jnp.float32)
        .at[asked.reshape(-1)]
        .add(returned.reshape(-1, feature))
    )
    table_part = lax.psum_scatter(dense, "dp", scatter_dimension=0, tiled=True)
    return (node_out[None, None], weight_grad, table_part[None])


def solution(mesh):
    return jax.shard_map(
        body,
        mesh=mesh,
        in_specs=(
            P("table", None),
            P(),
            P("dp", "table", None, None),
            P("dp", "table", None),
            P("dp", "table", None),
            P("dp", "table", None, None, None),
            P("dp", "table", None, None),
            P("dp", "table", None),
            P("dp", "table", None, None, None),
            P("dp", "table", None, None),
            P("dp", "table", None, None),
        ),
        out_specs=(P("dp", "table", None, None), P(), P("table", "dp", None)),
        check_vma=False,
    )
```

profile of v0, /device:TPU:0, one launch (start us, length us, event | category | flops | bytes accessed | tf_op | source)
XLA Modules:
  0.0 262.6 jit_solution(11616878313008494928)
XLA Ops:
  8.0 5.3 %all-to-all-start = ((s32[8,1,32]{2,1,0:T(1,128)}), s32[8,1,32]{2,1,0:T(1,128)S(1)}, u32[]{:S(2)}, u32[]{:S(2)}) async-start(s32[8,1,32]{2,1,0:T(1,128)} %bitcast.161), calls=%async_computation | async-start | bytes 8192 | tf_op jit(solution)/shard_map/all_to_all | solution.py:85
  13.4 1.4 convolution_bitcast_fusion.1
  14.8 1.1 fusion.30
  16.2 22.4 %while.42 = (s32[]{:T(128)}, f32[256,256]{1,0:T(8,128)S(1)}, s32[5,128,4]{2,1,0:T(8,128)S(1)}, s32[5,128]{1,0:T(8,128)S(1)}, f32[5,128,256]{1,2,0:T(8,128)S(1)}, /*index=5*/s32[]{:T(128)}, f32[]{:T(128)}) while((s32[]{:T(128)}, f32[256,256]{1,0:T(8,128)S(1)}, s32[5,128,4]{2,1,0:T(8,128)S(1)}, s32[5,128]{1,0:T(8,128)S(1)}, ...), condition=%wide.region_8.9_spmd, body=%wide.region_6.8_spmd.sunk | while | flops 297090 | bytes 3293797 | solution.py:29
  17.1 3.6 %scatter_custom_fusion.13 = f32[256,256]{1,0:T(8,128)S(1)} fusion(f32[256,256]{1,0:T(8,128)S(1)} %get-tuple-element.320, s32[512]{0:T(512)S(1)} %bitcast.155, f32[512,256]{1,0:T(8,128)S(1)} %broadcast_in_dim.194, f32[]{:T(128)} %constant.66.clone.1..sunk, pred[512]{0:T(512)(128)(4,1)S(1)} %lt.237), kind=kCustom, calls=%fused_computation.27.clone.1 | custom fusion | flops 262144 | bytes 786948 | tf_op jit(solution)/shard_map/while/body/eval_jaxpr/scatter-add | solution.py:26
  21.6 3.6 %scatter_custom_fusion.13 = f32[256,256]{1,0:T(8,128)S(1)} fusion(f32[256,256]{1,0:T(8,128)S(1)} %get-tuple-element.320, s32[512]{0:T(512)S(1)} %bitcast.155, f32[512,256]{1,0:T(8,128)S(1)} %broadcast_in_dim.194, f32[]{:T(128)} %constant.66.clone.1..sunk, pred[512]{0:T(512)(128)(4,1)S(1)} %lt.237), kind=kCustom, calls=%fused_computation.27.clone.1 | custom fusion | flops 262144 | bytes 786948 | tf_op jit(solution)/shard_map/while/body/eval_jaxpr/scatter-add | solution.py:26
  26.1 3.6 %scatter_custom_fusion.13 = f32[256,256]{1,0:T(8,128)S(1)} fusion(f32[256,256]{1,0:T(8,128)S(1)} %get-tuple-element.320, s32[512]{0:T(512)S(1)} %bitcast.155, f32[512,256]{1,0:T(8,128)S(1)} %broadcast_in_dim.194, f32[]{:T(128)} %constant.66.clone.1..sunk, pred[512]{0:T(512)(128)(4,1)S(1)} %lt.237), kind=kCustom, calls=%fused_computation.27.clone.1 | custom fusion | flops 262144 | bytes 786948 | tf_op jit(solution)/shard_map/while/body/eval_jaxpr/scatter-add | solution.py:26
  30.6 3.6 %scatter_custom_fusion.13 = f32[256,256]{1,0:T(8,128)S(1)} fusion(f32[256,256]{1,0:T(8,128)S(1)} %get-tuple-element.320, s32[512]{0:T(512)S(1)} %bitcast.155, f32[512,256]{1,0:T(8,128)S(1)} %broadcast_in_dim.194, f32[]{:T(128)} %constant.66.clone.1..sunk, pred[512]{0:T(512)(128)(4,1)S(1)} %lt.237), kind=kCustom, calls=%fused_computation.27.clone.1 | custom fusion | flops 262144 | bytes 786948 | tf_op jit(solution)/shard_map/while/body/eval_jaxpr/scatter-add | solution.py:26
  35.0 3.6 %scatter_custom_fusion.13 = f32[256,256]{1,0:T(8,128)S(1)} fusion(f32[256,256]{1,0:T(8,128)S(1)} %get-tuple-element.320, s32[512]{0:T(512)S(1)} %bitcast.155, f32[512,256]{1,0:T(8,128)S(1)} %broadcast_in_dim.194, f32[]{:T(128)} %constant.66.clone.1..sunk, pred[512]{0:T(512)(128)(4,1)S(1)} %lt.237), kind=kCustom, calls=%fused_computation.27.clone.1 | custom fusion | flops 262144 | bytes 786948 | tf_op jit(solution)/shard_map/while/body/eval_jaxpr/scatter-add | solution.py:26
  38.8 1.8 gather_fusion.2
  40.6 4.2 %all-to-all-start.1 = ((bf16[8,32,256]{2,1,0:T(8,128)(2,1)}), bf16[8,32,256]{2,1,0:T(8,128)(2,1)S(1)}, u32[]{:S(2)}, u32[]{:S(2)}) async-start(bf16[8,32,256]{2,1,0:T(8,128)(2,1)} %bitcast.15), calls=%async_computation.1 | async-start | bytes 262144 | tf_op jit(solution)/shard_map/all_to_all | solution.py:88
  45.8 1.6 scatter_fusion
  47.4 2.9 %all-to-all-done.1 = bf16[8,32,256]{2,1,0:T(8,128)(2,1)S(1)} async-done(((bf16[8,32,256]{2,1,0:T(8,128)(2,1)}), bf16[8,32,256]{2,1,0:T(8,128)(2,1)S(1)}, u32[]{:S(2)}, u32[]{:S(2)}) %all-to-all-start.1) | async-done | bytes 131104 | tf_op jit(solution)/shard_map/all_to_all | solution.py:88
  50.5 33.3 %while.40 = (s32[]{:T(128)}, bf16[5,256,256]{2,1,0:T(8,128)(2,1)}, s32[5,256]{1,0:T(8,128)S(1)}, s32[5,256,4]{2,1,0:T(8,128)S(1)}, bf16[256,256]{1,0:T(8,128)(2,1)S(1)}, /*index=5*/s32[]{:T(128)}) while((s32[]{:T(128)}, bf16[5,256,256]{2,1,0:T(8,128)(2,1)}, s32[5,256]{1,0:T(8,128)S(1)}, s32[5,256,4]{2,1,0:T(8,128)S(1)}, ...), condition=%wide.region_2.3_spmd, body=%wide.region_0.2_spmd.sunk | while | flops 857346 | bytes 3313753 | solution.py:16
  50.6 3.9 %gather_fusion = bf16[1024,256]{1,0:T(8,128)(2,1)S(1)} fusion(bf16[256,256]{1,0:T(8,128)(2,1)S(1)} %get-tuple-element.349, s32[1024]{0:T(1024)S(1)} %broadcast_clamp_fusion.2), kind=kCustom, calls=%fused_computation.clone.1 | custom fusion | bytes 1052672 | tf_op jit(solution)/shard_map/while/body/eval_jaxpr/gather | solution.py:12
  54.8 1.5 convert_reduce_fusion.4
  57.3 3.9 %gather_fusion = bf16[1024,256]{1,0:T(8,128)(2,1)S(1)} fusion(bf16[256,256]{1,0:T(8,128)(2,1)S(1)} %get-tuple-element.349, s32[1024]{0:T(1024)S(1)} %broadcast_clamp_fusion.2), kind=kCustom, calls=%fused_computation.clone.1 | custom fusion | bytes 1052672 | tf_op jit(solution)/shard_map/while/body/eval_jaxpr/gather | solution.py:12
  61.5 1.5 convert_reduce_fusion.4
  63.9 3.9 %gather_fusion = bf16[1024,256]{1,0:T(8,128)(2,1)S(1)} fusion(bf16[256,256]{1,0:T(8,128)(2,1)S(1)} %get-tuple-element.349, s32[1024]{0:T(1024)S(1)} %broadcast_clamp_fusion.2), kind=kCustom, calls=%fused_computation.clone.1 | custom fusion | bytes 1052672 | tf_op jit(solution)/shard_map/while/body/eval_jaxpr/gather | solution.py:12
  68.1 1.5 convert_reduce_fusion.4
  70.6 3.9 %gather_fusion = bf16[1024,256]{1,0:T(8,128)(2,1)S(1)} fusion(bf16[256,256]{1,0:T(8,128)(2,1)S(1)} %get-tuple-element.349, s32[1024]{0:T(1024)S(1)} %broadcast_clamp_fusion.2), kind=kCustom, calls=%fused_computation.clone.1 | custom fusion | bytes 1052672 | tf_op jit(solution)/shard_map/while/body/eval_jaxpr/gather | solution.py:12
  74.8 1.5 convert_reduce_fusion.4
  77.2 3.9 %gather_fusion = bf16[1024,256]{1,0:T(8,128)(2,1)S(1)} fusion(bf16[256,256]{1,0:T(8,128)(2,1)S(1)} %get-tuple-element.349, s32[1024]{0:T(1024)S(1)} %broadcast_clamp_fusion.2), kind=kCustom, calls=%fused_computation.clone.1 | custom fusion | bytes 1052672 | tf_op jit(solution)/shard_map/while/body/eval_jaxpr/gather | solution.py:12
  81.4 1.5 convert_reduce_fusion.4
  83.7 1.6 convolution_bitcast_fusion.4
  85.3 1.2 gather_fusion.3
  86.5 1.3 multiply_convert_fusion
  89.1 2.6 convolution_bitcast_fusion
  91.7 17.2 %while.41 = (s32[]{:T(128)}, bf16[5,128,256]{2,1,0:T(8,128)(2,1)}, s32[5,128]{1,0:T(8,128)S(1)}, s32[5,128,4]{2,1,0:T(8,128)S(1)}, bf16[256,256]{1,0:T(8,128)(2,1)S(1)}, /*index=5*/s32[]{:T(128)}) while((s32[]{:T(128)}, bf16[5,128,256]{2,1,0:T(8,128)(2,1)}, s32[5,128]{1,0:T(8,128)S(1)}, s32[5,128,4]{2,1,0:T(8,128)S(1)}, ...), condition=%wide.region_5.6_spmd, body=%wide.region_3.5_spmd.sunk | while | flops 429186 | bytes 1658457 | solution.py:16
  91.8 2.0 gather_fusion.1
  95.2 2.0 gather_fusion.1
  98.7 2.0 gather_fusion.1
  102.1 2.0 gather_fusion.1
  105.5 2.0 gather_fusion.1
  109.7 1.3 fusion.40
  111.3 1.9 maximum_bitcast_fusion
  113.2 44.2 %while.43 = (s32[]{:T(128)}, f32[256,256]{1,0:T(8,128)S(1)}, s32[5,256,4]{2,1,0:T(8,128)S(1)}, s32[5,256]{1,0:T(8,128)S(1)}, f32[5,256,256]{2,1,0:T(8,128)}, /*index=5*/s32[]{:T(128)}, f32[]{:T(128)}) while((s32[]{:T(128)}, f32[256,256]{1,0:T(8,128)S(1)}, s32[5,256,4]{2,1,0:T(8,128)S(1)}, s32[5,256]{1,0:T(8,128)S(1)}, ...), condition=%wide.region_14.15_spmd, body=%wide.region_12.14_spmd.sunk | while | flops 594178 | bytes 5277797 | solution.py:29
  115.3 6.8 %scatter_custom_fusion.15 = f32[256,256]{1,0:T(8,128)S(1)} fusion(f32[256,256]{1,0:T(8,128)S(1)} %get-tuple-element.377, s32[1024]{0:T(1024)S(1)} %bitcast.154, f32[1024,256]{1,0:T(8,128)S(1)} %broadcast_in_dim.198, f32[]{:T(128)} %constant.66.clone.1..sunk.1, pred[1024]{0:T(1024)(128)(4,1)S(1)} %lt.241), kind=kCustom, calls=%fused_computation.38.clone.1 | custom fusion | flops 524288 | bytes 1311748 | tf_op jit(solution)/shard_map/while/body/eval_jaxpr/scatter-add | solution.py:26
  124.1 6.8 %scatter_custom_fusion.15 = f32[256,256]{1,0:T(8,128)S(1)} fusion(f32[256,256]{1,0:T(8,128)S(1)} %get-tuple-element.377, s32[1024]{0:T(1024)S(1)} %bitcast.154, f32[1024,256]{1,0:T(8,128)S(1)} %broadcast_in_dim.198, f32[]{:T(128)} %constant.66.clone.1..sunk.1, pred[1024]{0:T(1024)(128)(4,1)S(1)} %lt.241), kind=kCustom, calls=%fused_computation.38.clone.1 | custom fusion | flops 524288 | bytes 1311748 | tf_op jit(solution)/shard_map/while/body/eval_jaxpr/scatter-add | solution.py:26
  133.0 6.8 %scatter_custom_fusion.15 = f32[256,256]{1,0:T(8,128)S(1)} fusion(f32[256,256]{1,0:T(8,128)S(1)} %get-tuple-element.377, s32[1024]{0:T(1024)S(1)} %bitcast.154, f32[1024,256]{1,0:T(8,128)S(1)} %broadcast_in_dim.198, f32[]{:T(128)} %constant.66.clone.1..sunk.1, pred[1024]{0:T(1024)(128)(4,1)S(1)} %lt.241), kind=kCustom, calls=%fused_computation.38.clone.1 | custom fusion | flops 524288 | bytes 1311748 | tf_op jit(solution)/shard_map/while/body/eval_jaxpr/scatter-add | solution.py:26
  141.8 6.8 %scatter_custom_fusion.15 = f32[256,256]{1,0:T(8,128)S(1)} fusion(f32[256,256]{1,0:T(8,128)S(1)} %get-tuple-element.377, s32[1024]{0:T(1024)S(1)} %bitcast.154, f32[1024,256]{1,0:T(8,128)S(1)} %broadcast_in_dim.198, f32[]{:T(128)} %constant.66.clone.1..sunk.1, pred[1024]{0:T(1024)(128)(4,1)S(1)} %lt.241), kind=kCustom, calls=%fused_computation.38.clone.1 | custom fusion | flops 524288 | bytes 1311748 | tf_op jit(solution)/shard_map/while/body/eval_jaxpr/scatter-add | solution.py:26
  150.7 6.8 %scatter_custom_fusion.15 = f32[256,256]{1,0:T(8,128)S(1)} fusion(f32[256,256]{1,0:T(8,128)S(1)} %get-tuple-element.377, s32[1024]{0:T(1024)S(1)} %bitcast.154, f32[1024,256]{1,0:T(8,128)S(1)} %broadcast_in_dim.198, f32[]{:T(128)} %constant.66.clone.1..sunk.1, pred[1024]{0:T(1024)(128)(4,1)S(1)} %lt.241), kind=kCustom, calls=%fused_computation.38.clone.1 | custom fusion | flops 524288 | bytes 1311748 | tf_op jit(solution)/shard_map/while/body/eval_jaxpr/scatter-add | solution.py:26
  158.6 2.1 scatter_fusion.1
  161.6 3.4 %all-to-all-start.2 = ((f32[8,32,256]{2,1,0:T(8,128)}), f32[8,32,256]{2,1,0:T(8,128)S(1)}, u32[]{:S(2)}, u32[]{:S(2)}) async-start(f32[8,32,256]{2,1,0:T(8,128)} %bitcast.41), calls=%async_computation.2 | async-start | bytes 524288 | tf_op jit(solution)/shard_map/all_to_all | solution.py:127
  166.3 6.1 %all-to-all-done.2 = f32[8,32,256]{2,1,0:T(8,128)S(1)} async-done(((f32[8,32,256]{2,1,0:T(8,128)}), f32[8,32,256]{2,1,0:T(8,128)S(1)}, u32[]{:S(2)}, u32[]{:S(2)}) %all-to-all-start.2) | async-done | bytes 262176 | tf_op jit(solution)/shard_map/all_to_all | solution.py:127
  172.3 2.7 %scatter_custom_fusion.4 = f32[512,256]{1,0:T(8,128)} fusion(s32[256]{0:T(256)S(1)} %bitcast.162, f32[256,256]{1,0:T(8,128)S(1)} %bitcast.149, f32[]{:T(128)} %constant.66.clone.1), kind=kCustom, calls=%fused_computation.69 | custom fusion | flops 65536 | bytes 524292 | tf_op jit(solution)/shard_map/scatter-add | solution.py:131
  176.2 75.6 %all-reduce.3.cloned.1.call-done = (f32[1,6,256,256]{3,2,1,0:T(8,128)}, f32[1,6,256,256]{3,2,1,0:T(8,128)}) async-done(((f32[1,6,256,256]{3,2,1,0:T(8,128)}, f32[1,6,256,256]{3,2,1,0:T(8,128)}), (f32[1,6,256,256]{3,2,1,0:T(8,128)}, f32[1,6,256,256]{3,2,1,0:T(8,128)})) %all-reduce.3.cloned.1.call-update) | async-done | bytes 3145744 | tf_op jit(solution)/shard_map/psum | solution.py:121
  251.8 3.4 %fusion.14 = bf16[2,6,256,256]{3,2,1,0:T(8,128)(2,1)} fusion(f32[1,6,256,256]{3,2,1,0:T(8,128)} %get-tuple-element.170, f32[1,6,256,256]{3,2,1,0:T(8,128)} %get-tuple-element.171), kind=kLoop, calls=%fused_computation.48 | loop fusion | flops 2359296 | bytes 4718592 | tf_op jit(solution)/shard_map/convert_element_type | solution.py:123
  (249 shorter events, 35.2 us)
Async XLA Ops:
  8.0 30.8 %copy-start = (bf16[512,256]{1,0:T(8,128)(2,1)S(1)}, bf16[512,256]{1,0:T(8,128)(2,1)}, u32[]{:S(2)}) copy-start(bf16[512,256]{1,0:T(8,128)(2,1)} %param.19) | copy-start | bytes 786436
  8.0 7.9 %copy-start.9 = (s32[1,1,5,128]{3,1,2,0:T(1,128)S(1)}, s32[1,1,5,128]{3,1,2,0:T(1,128)}, u32[]{:S(2)}) copy-start(s32[1,1,5,128]{3,1,2,0:T(1,128)} %param.28) | copy-start | bytes 7684
  8.0 7.9 %copy-start.7 = (s32[1,1,5,128,4]{3,4,2,1,0:T(4,128)S(1)}, s32[1,1,5,128,4]{3,4,2,1,0:T(4,128)}, u32[]{:S(2)}) copy-start(s32[1,1,5,128,4]{3,4,2,1,0:T(4,128)} %param.27) | copy-start | bytes 30724
  8.0 30.7 %all-to-all-start = ((s32[8,1,32]{2,1,0:T(1,128)}), s32[8,1,32]{2,1,0:T(1,128)S(1)}, u32[]{:S(2)}, u32[]{:S(2)}) async-start(s32[8,1,32]{2,1,0:T(1,128)} %bitcast.161), calls=%async_computation | async-start | bytes 8192 | tf_op jit(solution)/shard_map/all_to_all | solution.py:85
  16.2 22.5 %copy-start.12 = (s32[1,1,8]{2,1,0:T(1,128)S(1)}, s32[1,1,8]{2,1,0:T(1,128)}, u32[]{:S(2)}) copy-start(s32[1,1,8]{2,1,0:T(1,128)} %param.22) | copy-start | bytes 100
  16.2 22.5 %copy-start.10 = (s32[1,1,256]{2,1,0:T(1,128)S(1)}, s32[1,1,256]{2,1,0:T(1,128)}, u32[]{:S(2)}) copy-start(s32[1,1,256]{2,1,0:T(1,128)} %param.23) | copy-start | bytes 3076
  16.2 22.5 %copy-start.13 = (s32[1,1,128]{2,1,0:T(1,128)S(1)}, s32[1,1,128]{2,1,0:T(1,128)}, u32[]{:S(2)}) copy-start(s32[1,1,128]{2,1,0:T(1,128)} %param.26) | copy-start | bytes 1540
  16.2 28.7 %copy-start.8 = (s32[1,1,5,256]{3,1,2,0:T(1,128)S(1)}, s32[1,1,5,256]{3,1,2,0:T(1,128)}, u32[]{:S(2)}) copy-start(s32[1,1,5,256]{3,1,2,0:T(1,128)} %param.25) | copy-start | bytes 15364
  16.2 28.7 %copy-start.6 = (s32[1,1,5,256,4]{3,4,2,1,0:T(4,128)S(1)}, s32[1,1,5,256,4]{3,4,2,1,0:T(4,128)}, u32[]{:S(2)}) copy-start(s32[1,1,5,256,4]{3,4,2,1,0:T(4,128)} %param.24) | copy-start | bytes 61444
  40.6 9.7 %all-to-all-start.1 = ((bf16[8,32,256]{2,1,0:T(8,128)(2,1)}), bf16[8,32,256]{2,1,0:T(8,128)(2,1)S(1)}, u32[]{:S(2)}, u32[]{:S(2)}) async-start(bf16[8,32,256]{2,1,0:T(8,128)(2,1)} %bitcast.15), calls=%async_computation.1 | async-start | bytes 262144 | tf_op jit(solution)/shard_map/all_to_all | solution.py:88
  44.8 206.9 %all-reduce.3.cloned.1.call-start = ((), (), s32[]{:S(2)}) async-start(), calls=%async_computation.5 | async-start | bytes 6291456 | tf_op jit(solution)/shard_map/psum | solution.py:121
  86.5 1.3 copy-start.4
  91.7 18.0 %copy-start.3 = (bf16[1,1,128,256]{3,2,1,0:T(8,128)(2,1)S(1)}, bf16[1,1,128,256]{3,2,1,0:T(8,128)(2,1)}, u32[]{:S(2)}) copy-start(bf16[1,1,128,256]{3,2,1,0:T(8,128)(2,1)} %param.29) | copy-start | bytes 196612
  108.9 2.4 copy-start.2
  158.6 2.1 copy-start.11
  160.7 14.4 %copy-start.1 = (bf16[2,6,256,256]{3,2,1,0:T(8,128)(2,1)S(1)}, bf16[2,6,256,256]{3,2,1,0:T(8,128)(2,1)}, u32[]{:S(2)}) copy-start(bf16[2,6,256,256]{3,2,1,0:T(8,128)(2,1)} %param.20) | copy-start | bytes 4718596
  160.7 14.4 %copy-start.5 = (bf16[5,128,256]{2,1,0:T(8,128)(2,1)S(1)}, bf16[5,128,256]{2,1,0:T(8,128)(2,1)}, u32[]{:S(2)}) copy-start(bf16[5,128,256]{2,1,0:T(8,128)(2,1)} %get-tuple-element.112) | copy-start | bytes 983044
  161.6 10.8 %all-to-all-start.2 = ((f32[8,32,256]{2,1,0:T(8,128)}), f32[8,32,256]{2,1,0:T(8,128)S(1)}, u32[]{:S(2)}, u32[]{:S(2)}) async-start(f32[8,32,256]{2,1,0:T(8,128)} %bitcast.41), calls=%async_computation.2 | async-start | bytes 524288 | tf_op jit(solution)/shard_map/all_to_all | solution.py:127
  165.0 90.2 %reduce-scatter.2.cloned.1.call-start = ((), (), s32[]{:S(2)}) async-start(), calls=%async_computation.4 | async-start | bytes 655360 | tf_op jit(solution)/shard_map/reduce_scatter | solution.py:133
Sparse Core Ops, SparseCore 0:
  113.3 138.4 all-reduce.2
Sparse Core Ops, SparseCore 1:
  175.2 21.4 reduce-scatter.1
where the time goes:
time: 263 us
  other arithmetic  90.3 us (34%)
  waiting for transfers between devices  84.6 us (32%)
  local copies, waits for them, and re-layouts  44.5 us (17%)
  between operations  15.9 us (6%)
  starting transfers between devices  13 us (5%)
  matrix products  13 us (5%)
    psum x1, waiting for transfers between devices, body(): grad_bottom, grad_top = lax.psum((grad_bottom, grad_top), ('dp', 'table'))  75.6 us
    scatter-add x10, other arithmetic, spread_single(): running.at[indices.reshape(-1)].add(placed.reshape(-1, part_grad.shape[-1]))  51.7 us
    gather x20, local copies, waits for them, and re-layouts, aggregate_single(): features[indices]  30.4 us
    reduce_sum x10, other arithmetic, aggregate_single(): summed = jnp.sum(picked.astype(jnp.float32), axis=1)  9.69 us
    dynamic_update_slice x10, other arithmetic, aggregate(): return lax.map(aggregate_single, (edges, degrees))  7.46 us
    all_to_all x1, waiting for transfers between devices, body(): lax.all_to_all(slot_grads, 'table', split_axis=0, concat_axis=0, tiled=True)  6.05 us
    div x10, other arithmetic, spread_single(): scaled = part_grad / degree[:, None].astype(part_grad.dtype)  5.76 us
    all_to_all x1, starting transfers between devices, body(): lax.all_to_all(wanted, 'table', split_axis=0, concat_axis=0, tiled=True)  5.34 us
  transfers between devices with their start and end apart: 5, of which 3 were waited for; matrix products, arithmetic and copies ran while one was open for 32% of the time, Pallas kernels for 0%

commit v1 on v0

--- a/solution.py
+++ b/solution.py
@@ -118,7 +118,7 @@
     )
     grad_slots = grad_slots + spread_back(rel_back, first_edges, first_degree, inputs.shape[0])
     grad_slots = jnp.where(living.reshape(-1)[:, None], grad_slots, jnp.zeros((), grad_slots.dtype))
-    grad_bottom, grad_top = lax.psum((grad_bottom, grad_top), ("dp", "table"))
+    grad_bottom, grad_top = lax.psum(lax.psum((grad_bottom, grad_top), "table"), "dp")
     seeds = cot_rows.shape[0] * lax.axis_size("dp") * lax.axis_size("table")
     weight_grad = (jnp.stack([grad_bottom, grad_top]) / jnp.sqrt(jnp.float32(seeds))).astype(
         jnp.bfloat16

time: 263 us -> 330 us (1.25)
  waiting for transfers between devices: 84.6 us -> 158 us
  other arithmetic: 90.3 us -> 86.9 us
    psum x1 -> x2, waiting for transfers between devices: 75.6 us -> 128 us  [the longest x1 65.8 us: body(): lax.psum((grad_bottom, grad_top), 'table')]
    reduce_scatter x1, waiting for transfers between devices: 0.01 us -> 20.4 us  [body(): table_part = lax.psum_scatter(dense, 'dp', scatter_dimension=0, tiled=True)]
    dynamic_update_slice x10, other arithmetic: 7.46 us -> 4.12 us  [aggregate(): return lax.map(aggregate_single, (edges, degrees))]
  transfers between devices with their start and end apart: 5 -> 6, of which waited for: 3 -> 5; matrix products, arithmetic and copies ran while one was open for 32% -> 25% of each run, Pallas kernels for 0% -> 0%
where the time goes in v1:
time: 330 us; the launch traced here: 329 us
  waiting for transfers between devices  158 us (48%)
  other arithmetic  86.9 us (26%)
  local copies, waits for them, and re-layouts  45 us (14%)
  between operations  14.2 us (4%)
  starting transfers between devices  13.3 us (4%)
  matrix products  11 us (3%)
    psum x1, waiting for transfers between devices, body(): lax.psum((grad_bottom, grad_top), 'table')  65.8 us
    psum x1, waiting for transfers between devices, body(): lax.psum(lax.psum((grad_bottom, grad_top), 'table'), 'dp')  62.1 us
    scatter-add x10, other arithmetic, spread_single(): running.at[indices.reshape(-1)].add(placed.reshape(-1, part_grad.shape[-1]))  51.7 us
    gather x20, local copies, waits for them, and re-layouts, aggregate_single(): features[indices]  30.4 us
    reduce_scatter x1, waiting for transfers between devices, body(): table_part = lax.psum_scatter(dense, 'dp', scatter_dimension=0, tiled=True)  20.4 us
    reduce_sum x10, other arithmetic, aggregate_single(): summed = jnp.sum(picked.astype(jnp.float32), axis=1)  9.68 us
  transfers between devices with their start and end apart: 6, of which 5 were waited for; matrix products, arithmetic and copies ran while one was open for 25% of the time, Pallas kernels for 0%

profile of v1, /device:TPU:0, one launch (start us, length us, event | category | flops | bytes accessed | tf_op | source)
XLA Modules:
  0.0 329.5 jit_solution(4129349528260238591)
XLA Ops:
  7.2 5.3 %all-to-all-start = ((s32[8,1,32]{2,1,0:T(1,128)}), s32[8,1,32]{2,1,0:T(1,128)S(1)}, u32[]{:S(2)}, u32[]{:S(2)}) async-start(s32[8,1,32]{2,1,0:T(1,128)} %bitcast.161), calls=%async_computation | async-start | bytes 8192 | tf_op jit(solution)/shard_map/all_to_all | solution.py:85
  12.5 1.4 convolution_bitcast_fusion.1
  15.4 22.4 %while.42 = (s32[]{:T(128)}, f32[256,256]{1,0:T(8,128)S(1)}, s32[5,128,4]{2,1,0:T(8,128)S(1)}, s32[5,128]{1,0:T(8,128)S(1)}, f32[5,128,256]{1,2,0:T(8,128)S(1)}, /*index=5*/s32[]{:T(128)}, f32[]{:T(128)}) while((s32[]{:T(128)}, f32[256,256]{1,0:T(8,128)S(1)}, s32[5,128,4]{2,1,0:T(8,128)S(1)}, s32[5,128]{1,0:T(8,128)S(1)}, ...), condition=%wide.region_8.9_spmd, body=%wide.region_6.8_spmd.sunk | while | flops 297090 | bytes 3293797 | solution.py:29
  16.3 3.6 %scatter_custom_fusion.13 = f32[256,256]{1,0:T(8,128)S(1)} fusion(f32[256,256]{1,0:T(8,128)S(1)} %get-tuple-element.322, s32[512]{0:T(512)S(1)} %bitcast.155, f32[512,256]{1,0:T(8,128)S(1)} %broadcast_in_dim.194, f32[]{:T(128)} %constant.66.clone.1..sunk, pred[512]{0:T(512)(128)(4,1)S(1)} %lt.237), kind=kCustom, calls=%fused_computation.27.clone.1 | custom fusion | flops 262144 | bytes 786948 | tf_op jit(solution)/shard_map/while/body/eval_jaxpr/scatter-add | solution.py:26
  20.8 3.6 %scatter_custom_fusion.13 = f32[256,256]{1,0:T(8,128)S(1)} fusion(f32[256,256]{1,0:T(8,128)S(1)} %get-tuple-element.322, s32[512]{0:T(512)S(1)} %bitcast.155, f32[512,256]{1,0:T(8,128)S(1)} %broadcast_in_dim.194, f32[]{:T(128)} %constant.66.clone.1..sunk, pred[512]{0:T(512)(128)(4,1)S(1)} %lt.237), kind=kCustom, calls=%fused_computation.27.clone.1 | custom fusion | flops 262144 | bytes 786948 | tf_op jit(solution)/shard_map/while/body/eval_jaxpr/scatter-add | solution.py:26
  25.2 3.6 %scatter_custom_fusion.13 = f32[256,256]{1,0:T(8,128)S(1)} fusion(f32[256,256]{1,0:T(8,128)S(1)} %get-tuple-element.322, s32[512]{0:T(512)S(1)} %bitcast.155, f32[512,256]{1,0:T(8,128)S(1)} %broadcast_in_dim.194, f32[]{:T(128)} %constant.66.clone.1..sunk, pred[512]{0:T(512)(128)(4,1)S(1)} %lt.237), kind=kCustom, calls=%fused_computation.27.clone.1 | custom fusion | flops 262144 | bytes 786948 | tf_op jit(solution)/shard_map/while/body/eval_jaxpr/scatter-add | solution.py:26
  29.7 3.6 %scatter_custom_fusion.13 = f32[256,256]{1,0:T(8,128)S(1)} fusion(f32[256,256]{1,0:T(8,128)S(1)} %get-tuple-element.322, s32[512]{0:T(512)S(1)} %bitcast.155, f32[512,256]{1,0:T(8,128)S(1)} %broadcast_in_dim.194, f32[]{:T(128)} %constant.66.clone.1..sunk, pred[512]{0:T(512)(128)(4,1)S(1)} %lt.237), kind=kCustom, calls=%fused_computation.27.clone.1 | custom fusion | flops 262144 | bytes 786948 | tf_op jit(solution)/shard_map/while/body/eval_jaxpr/scatter-add | solution.py:26
  34.2 3.6 %scatter_custom_fusion.13 = f32[256,256]{1,0:T(8,128)S(1)} fusion(f32[256,256]{1,0:T(8,128)S(1)} %get-tuple-element.322, s32[512]{0:T(512)S(1)} %bitcast.155, f32[512,256]{1,0:T(8,128)S(1)} %broadcast_in_dim.194, f32[]{:T(128)} %constant.66.clone.1..sunk, pred[512]{0:T(512)(128)(4,1)S(1)} %lt.237), kind=kCustom, calls=%fused_computation.27.clone.1 | custom fusion | flops 262144 | bytes 786948 | tf_op jit(solution)/shard_map/while/body/eval_jaxpr/scatter-add | solution.py:26
  38.0 1.8 gather_fusion.2
  39.8 4.2 %all-to-all-start.1 = ((bf16[8,32,256]{2,1,0:T(8,128)(2,1)}), bf16[8,32,256]{2,1,0:T(8,128)(2,1)S(1)}, u32[]{:S(2)}, u32[]{:S(2)}) async-start(bf16[8,32,256]{2,1,0:T(8,128)(2,1)} %bitcast.15), calls=%async_computation.1 | async-start | bytes 262144 | tf_op jit(solution)/shard_map/all_to_all | solution.py:88
  44.4 1.4 scatter_fusion
  45.8 3.7 %all-to-all-done.1 = bf16[8,32,256]{2,1,0:T(8,128)(2,1)S(1)} async-done(((bf16[8,32,256]{2,1,0:T(8,128)(2,1)}), bf16[8,32,256]{2,1,0:T(8,128)(2,1)S(1)}, u32[]{:S(2)}, u32[]{:S(2)}) %all-to-all-start.1) | async-done | bytes 131104 | tf_op jit(solution)/shard_map/all_to_all | solution.py:88
  49.7 30.1 %while.40 = (s32[]{:T(128)}, bf16[5,256,256]{2,1,0:T(8,128)(2,1)S(1)}, s32[5,256]{1,0:T(8,128)S(1)}, s32[5,256,4]{2,1,0:T(8,128)S(1)}, bf16[256,256]{1,0:T(8,128)(2,1)S(1)}, /*index=5*/s32[]{:T(128)}) while((s32[]{:T(128)}, bf16[5,256,256]{2,1,0:T(8,128)(2,1)S(1)}, s32[5,256]{1,0:T(8,128)S(1)}, s32[5,256,4]{2,1,0:T(8,128)S(1)}, ...), condition=%wide.region_2.3_spmd, body=%wide.region_0.2_spmd.sunk | while | flops 857346 | bytes 3313753 | solution.py:16
  49.8 3.9 %gather_fusion = bf16[1024,256]{1,0:T(8,128)(2,1)S(1)} fusion(bf16[256,256]{1,0:T(8,128)(2,1)S(1)} %get-tuple-element.351, s32[1024]{0:T(1024)S(1)} %broadcast_clamp_fusion.2), kind=kCustom, calls=%fused_computation.clone.1 | custom fusion | bytes 1052672 | tf_op jit(solution)/shard_map/while/body/eval_jaxpr/gather | solution.py:12
  54.0 1.5 convert_reduce_fusion.4
  55.8 3.9 %gather_fusion = bf16[1024,256]{1,0:T(8,128)(2,1)S(1)} fusion(bf16[256,256]{1,0:T(8,128)(2,1)S(1)} %get-tuple-element.351, s32[1024]{0:T(1024)S(1)} %broadcast_clamp_fusion.2), kind=kCustom, calls=%fused_computation.clone.1 | custom fusion | bytes 1052672 | tf_op jit(solution)/shard_map/while/body/eval_jaxpr/gather | solution.py:12
  60.0 1.5 convert_reduce_fusion.4
  61.9 3.9 %gather_fusion = bf16[1024,256]{1,0:T(8,128)(2,1)S(1)} fusion(bf16[256,256]{1,0:T(8,128)(2,1)S(1)} %get-tuple-element.351, s32[1024]{0:T(1024)S(1)} %broadcast_clamp_fusion.2), kind=kCustom, calls=%fused_computation.clone.1 | custom fusion | bytes 1052672 | tf_op jit(solution)/shard_map/while/body/eval_jaxpr/gather | solution.py:12
  66.1 1.5 convert_reduce_fusion.4
  67.9 3.9 %gather_fusion = bf16[1024,256]{1,0:T(8,128)(2,1)S(1)} fusion(bf16[256,256]{1,0:T(8,128)(2,1)S(1)} %get-tuple-element.351, s32[1024]{0:T(1024)S(1)} %broadcast_clamp_fusion.2), kind=kCustom, calls=%fused_computation.clone.1 | custom fusion | bytes 1052672 | tf_op jit(solution)/shard_map/while/body/eval_jaxpr/gather | solution.py:12
  72.1 1.5 convert_reduce_fusion.4
  73.9 3.9 %gather_fusion = bf16[1024,256]{1,0:T(8,128)(2,1)S(1)} fusion(bf16[256,256]{1,0:T(8,128)(2,1)S(1)} %get-tuple-element.351, s32[1024]{0:T(1024)S(1)} %broadcast_clamp_fusion.2), kind=kCustom, calls=%fused_computation.clone.1 | custom fusion | bytes 1052672 | tf_op jit(solution)/shard_map/while/body/eval_jaxpr/gather | solution.py:12
  78.1 1.5 convert_reduce_fusion.4
  79.8 1.7 convolution_bitcast_fusion.4
  82.6 1.3 multiply_convert_fusion
  85.2 17.1 %while.41 = (s32[]{:T(128)}, bf16[5,128,256]{2,1,0:T(8,128)(2,1)}, s32[5,128]{1,0:T(8,128)S(1)}, s32[5,128,4]{2,1,0:T(8,128)S(1)}, bf16[256,256]{1,0:T(8,128)(2,1)S(1)}, /*index=5*/s32[]{:T(128)}) while((s32[]{:T(128)}, bf16[5,128,256]{2,1,0:T(8,128)(2,1)}, s32[5,128]{1,0:T(8,128)S(1)}, s32[5,128,4]{2,1,0:T(8,128)S(1)}, ...), condition=%wide.region_5.6_spmd, body=%wide.region_3.5_spmd.sunk | while | flops 429186 | bytes 1658457 | solution.py:16
  85.3 2.0 gather_fusion.1
  88.8 2.0 gather_fusion.1
  92.2 2.0 gather_fusion.1
  95.6 2.0 gather_fusion.1
  99.0 2.0 gather_fusion.1
  103.2 1.3 fusion.40
  104.8 2.0 pad_maximum_fusion
  108.4 1.4 convolution_bitcast_fusion
  109.8 65.8 %all-reduce.5.cloned.1.call-done = (f32[6,256,256]{2,1,0:T(8,128)}, f32[6,256,256]{2,1,0:T(8,128)}) async-done(((f32[6,256,256]{2,1,0:T(8,128)}, f32[6,256,256]{2,1,0:T(8,128)}), (f32[6,256,256]{2,1,0:T(8,128)}, f32[6,256,256]{2,1,0:T(8,128)})) %all-reduce.5.cloned.1.call-update) | async-done | bytes 3145744 | tf_op jit(solution)/shard_map/psum | solution.py:121
  175.7 44.2 %while.43 = (s32[]{:T(128)}, f32[256,256]{1,0:T(8,128)S(1)}, s32[5,256,4]{2,1,0:T(8,128)S(1)}, s32[5,256]{1,0:T(8,128)S(1)}, f32[5,256,256]{2,1,0:T(8,128)}, /*index=5*/s32[]{:T(128)}, f32[]{:T(128)}) while((s32[]{:T(128)}, f32[256,256]{1,0:T(8,128)S(1)}, s32[5,256,4]{2,1,0:T(8,128)S(1)}, s32[5,256]{1,0:T(8,128)S(1)}, ...), condition=%wide.region_16.17_spmd, body=%wide.region_14.16_spmd.sunk | while | flops 594178 | bytes 5277797 | solution.py:29
  177.7 6.8 %scatter_custom_fusion.15 = f32[256,256]{1,0:T(8,128)S(1)} fusion(f32[256,256]{1,0:T(8,128)S(1)} %get-tuple-element.379, s32[1024]{0:T(1024)S(1)} %bitcast.154, f32[1024,256]{1,0:T(8,128)S(1)} %broadcast_in_dim.198, f32[]{:T(128)} %constant.66.clone.1..sunk.1, pred[1024]{0:T(1024)(128)(4,1)S(1)} %lt.241), kind=kCustom, calls=%fused_computation.38.clone.1 | custom fusion | flops 524288 | bytes 1311748 | tf_op jit(solution)/shard_map/while/body/eval_jaxpr/scatter-add | solution.py:26
  186.6 6.8 %scatter_custom_fusion.15 = f32[256,256]{1,0:T(8,128)S(1)} fusion(f32[256,256]{1,0:T(8,128)S(1)} %get-tuple-element.379, s32[1024]{0:T(1024)S(1)} %bitcast.154, f32[1024,256]{1,0:T(8,128)S(1)} %broadcast_in_dim.198, f32[]{:T(128)} %constant.66.clone.1..sunk.1, pred[1024]{0:T(1024)(128)(4,1)S(1)} %lt.241), kind=kCustom, calls=%fused_computation.38.clone.1 | custom fusion | flops 524288 | bytes 1311748 | tf_op jit(solution)/shard_map/while/body/eval_jaxpr/scatter-add | solution.py:26
  195.4 6.8 %scatter_custom_fusion.15 = f32[256,256]{1,0:T(8,128)S(1)} fusion(f32[256,256]{1,0:T(8,128)S(1)} %get-tuple-element.379, s32[1024]{0:T(1024)S(1)} %bitcast.154, f32[1024,256]{1,0:T(8,128)S(1)} %broadcast_in_dim.198, f32[]{:T(128)} %constant.66.clone.1..sunk.1, pred[1024]{0:T(1024)(128)(4,1)S(1)} %lt.241), kind=kCustom, calls=%fused_computation.38.clone.1 | custom fusion | flops 524288 | bytes 1311748 | tf_op jit(solution)/shard_map/while/body/eval_jaxpr/scatter-add | solution.py:26
  204.3 6.8 %scatter_custom_fusion.15 = f32[256,256]{1,0:T(8,128)S(1)} fusion(f32[256,256]{1,0:T(8,128)S(1)} %get-tuple-element.379, s32[1024]{0:T(1024)S(1)} %bitcast.154, f32[1024,256]{1,0:T(8,128)S(1)} %broadcast_in_dim.198, f32[]{:T(128)} %constant.66.clone.1..sunk.1, pred[1024]{0:T(1024)(128)(4,1)S(1)} %lt.241), kind=kCustom, calls=%fused_computation.38.clone.1 | custom fusion | flops 524288 | bytes 1311748 | tf_op jit(solution)/shard_map/while/body/eval_jaxpr/scatter-add | solution.py:26
  213.1 6.8 %scatter_custom_fusion.15 = f32[256,256]{1,0:T(8,128)S(1)} fusion(f32[256,256]{1,0:T(8,128)S(1)} %get-tuple-element.379, s32[1024]{0:T(1024)S(1)} %bitcast.154, f32[1024,256]{1,0:T(8,128)S(1)} %broadcast_in_dim.198, f32[]{:T(128)} %constant.66.clone.1..sunk.1, pred[1024]{0:T(1024)(128)(4,1)S(1)} %lt.241), kind=kCustom, calls=%fused_computation.38.clone.1 | custom fusion | flops 524288 | bytes 1311748 | tf_op jit(solution)/shard_map/while/body/eval_jaxpr/scatter-add | solution.py:26
  219.9 2.2 scatter_fusion.1
  223.0 3.4 %all-to-all-start.2 = ((f32[8,32,256]{2,1,0:T(8,128)}), f32[8,32,256]{2,1,0:T(8,128)S(1)}, u32[]{:S(2)}, u32[]{:S(2)}) async-start(f32[8,32,256]{2,1,0:T(8,128)} %bitcast.41), calls=%async_computation.2 | async-start | bytes 524288 | tf_op jit(solution)/shard_map/all_to_all | solution.py:127
  227.7 5.5 %all-to-all-done.2 = f32[8,32,256]{2,1,0:T(8,128)S(1)} async-done(((f32[8,32,256]{2,1,0:T(8,128)}), f32[8,32,256]{2,1,0:T(8,128)S(1)}, u32[]{:S(2)}, u32[]{:S(2)}) %all-to-all-start.2) | async-done | bytes 262176 | tf_op jit(solution)/shard_map/all_to_all | solution.py:127
  233.3 2.7 scatter_custom_fusion.4
  237.1 62.1 %all-reduce.7.cloned.1.call-done = (f32[1,6,256,256]{3,2,1,0:T(8,128)}, f32[1,6,256,256]{3,2,1,0:T(8,128)}) async-done(((f32[1,6,256,256]{3,2,1,0:T(8,128)}, f32[1,6,256,256]{3,2,1,0:T(8,128)}), (f32[1,6,256,256]{3,2,1,0:T(8,128)}, f32[1,6,256,256]{3,2,1,0:T(8,128)})) %all-reduce.7.cloned.1.call-update) | async-done | bytes 3145744 | tf_op jit(solution)/shard_map/psum | solution.py:121
  299.2 3.4 %fusion.14 = bf16[2,6,256,256]{3,2,1,0:T(8,128)(2,1)} fusion(f32[1,6,256,256]{3,2,1,0:T(8,128)} %get-tuple-element.172, f32[1,6,256,256]{3,2,1,0:T(8,128)} %get-tuple-element.173), kind=kLoop, calls=%fused_computation.48 | loop fusion | flops 2359296 | bytes 4718592 | tf_op jit(solution)/shard_map/convert_element_type | solution.py:123
  302.6 20.4 %reduce-scatter.2.cloned.1.call-done = f32[128,256]{1,0:T(8,128)} async-done(((f32[512,256]{1,0:T(8,128)}), f32[128,256]{1,0:T(8,128)}) %reduce-scatter.2.cloned.1.call-update) | async-done | bytes 131088 | tf_op jit(solution)/shard_map/reduce_scatter | solution.py:133
  (266 shorter events, 34.0 us)
Async XLA Ops:
  7.2 30.9 %copy-start = (bf16[512,256]{1,0:T(8,128)(2,1)S(1)}, bf16[512,256]{1,0:T(8,128)(2,1)}, u32[]{:S(2)}) copy-start(bf16[512,256]{1,0:T(8,128)(2,1)} %param.19) | copy-start | bytes 786436
  7.2 7.9 %copy-start.16 = (s32[1,1,5,128]{3,1,2,0:T(1,128)S(1)}, s32[1,1,5,128]{3,1,2,0:T(1,128)}, u32[]{:S(2)}) copy-start(s32[1,1,5,128]{3,1,2,0:T(1,128)} %param.28) | copy-start | bytes 7684
  7.2 7.9 %copy-start.13 = (s32[1,1,5,128,4]{3,4,2,1,0:T(4,128)S(1)}, s32[1,1,5,128,4]{3,4,2,1,0:T(4,128)}, u32[]{:S(2)}) copy-start(s32[1,1,5,128,4]{3,4,2,1,0:T(4,128)} %param.27) | copy-start | bytes 30724
  7.2 30.7 %all-to-all-start = ((s32[8,1,32]{2,1,0:T(1,128)}), s32[8,1,32]{2,1,0:T(1,128)S(1)}, u32[]{:S(2)}, u32[]{:S(2)}) async-start(s32[8,1,32]{2,1,0:T(1,128)} %bitcast.161), calls=%async_computation | async-start | bytes 8192 | tf_op jit(solution)/shard_map/all_to_all | solution.py:85
  15.3 22.5 %copy-start.19 = (s32[1,1,8]{2,1,0:T(1,128)S(1)}, s32[1,1,8]{2,1,0:T(1,128)}, u32[]{:S(2)}) copy-start(s32[1,1,8]{2,1,0:T(1,128)} %param.22) | copy-start | bytes 100
  15.4 22.5 %copy-start.17 = (s32[1,1,256]{2,1,0:T(1,128)S(1)}, s32[1,1,256]{2,1,0:T(1,128)}, u32[]{:S(2)}) copy-start(s32[1,1,256]{2,1,0:T(1,128)} %param.23) | copy-start | bytes 3076
  15.4 22.5 %copy-start.20 = (s32[1,1,128]{2,1,0:T(1,128)S(1)}, s32[1,1,128]{2,1,0:T(1,128)}, u32[]{:S(2)}) copy-start(s32[1,1,128]{2,1,0:T(1,128)} %param.26) | copy-start | bytes 1540
  15.4 28.7 %copy-start.15 = (s32[1,1,5,256]{3,1,2,0:T(1,128)S(1)}, s32[1,1,5,256]{3,1,2,0:T(1,128)}, u32[]{:S(2)}) copy-start(s32[1,1,5,256]{3,1,2,0:T(1,128)} %param.25) | copy-start | bytes 15364
  15.4 28.8 %copy-start.12 = (s32[1,1,5,256,4]{3,4,2,1,0:T(4,128)S(1)}, s32[1,1,5,256,4]{3,4,2,1,0:T(4,128)}, u32[]{:S(2)}) copy-start(s32[1,1,5,256,4]{3,4,2,1,0:T(4,128)} %param.24) | copy-start | bytes 61444
  37.9 11.8 %copy-start.14 = (s32[256,1]{0,1:T(1,128)}, s32[256,1]{0,1:T(1,128)S(1)}, u32[]{:S(2)}) copy-start(s32[256,1]{0,1:T(1,128)S(1)} %compare_select_fusion.6) | copy-start | bytes 3076
  37.9 6.2 %copy-start.10 = (s32[8,1,32]{2,1,0:T(1,128)}, s32[8,1,32]{2,1,0:T(1,128)S(1)}, u32[]{:S(2)}) copy-start(s32[8,1,32]{2,1,0:T(1,128)S(1)} %all-to-all-done) | copy-start | bytes 3076
  39.8 9.7 %all-to-all-start.1 = ((bf16[8,32,256]{2,1,0:T(8,128)(2,1)}), bf16[8,32,256]{2,1,0:T(8,128)(2,1)S(1)}, u32[]{:S(2)}, u32[]{:S(2)}) async-start(bf16[8,32,256]{2,1,0:T(8,128)(2,1)} %bitcast.15), calls=%async_computation.1 | async-start | bytes 262144 | tf_op jit(solution)/shard_map/all_to_all | solution.py:88
  44.0 131.6 %all-reduce.5.cloned.1.call-start = ((), (), s32[]{:S(2)}) async-start(), calls=%async_computation.5 | async-start | bytes 6291456 | tf_op jit(solution)/shard_map/psum | solution.py:121
  79.7 1.7 copy-start.5
  82.6 1.3 copy-start.6
  85.2 18.0 %copy-start.4 = (bf16[1,1,128,256]{3,2,1,0:T(8,128)(2,1)S(1)}, bf16[1,1,128,256]{3,2,1,0:T(8,128)(2,1)}, u32[]{:S(2)}) copy-start(bf16[1,1,128,256]{3,2,1,0:T(8,128)(2,1)} %param.29) | copy-start | bytes 196612
  102.3 2.4 copy-start.3
  103.2 3.6 %copy-start.7 = (bf16[128,256]{1,0:T(8,128)(2,1)}, bf16[128,256]{1,0:T(8,128)(2,1)S(1)}, u32[]{:S(2)}) copy-start(bf16[128,256]{1,0:T(8,128)(2,1)S(1)} %gather_fusion.4) | copy-start | bytes 196612
  106.8 1.4 copy-start.1
  106.8 192.4 %all-reduce.7.cloned.1.call-start = ((), (), s32[]{:S(2)}) async-start(), calls=%async_computation.6 | async-start | bytes 6291456 | tf_op jit(solution)/shard_map/psum | solution.py:121
  219.9 2.2 copy-start.18
  219.9 7.1 %copy-start.11 = (s32[8,1,32]{2,1,0:T(1,128)S(1)}, s32[8,1,32]{2,1,0:T(1,128)}, u32[]{:S(2)}) copy-start(s32[8,1,32]{2,1,0:T(1,128)} %copy-done.10) | copy-start | bytes 3076
  222.2 13.9 %copy-start.2 = (bf16[2,6,256,256]{3,2,1,0:T(8,128)(2,1)S(1)}, bf16[2,6,256,256]{3,2,1,0:T(8,128)(2,1)}, u32[]{:S(2)}) copy-start(bf16[2,6,256,256]{3,2,1,0:T(8,128)(2,1)} %param.20) | copy-start | bytes 4718596
  222.2 13.9 %copy-start.9 = (bf16[5,128,256]{2,1,0:T(8,128)(2,1)S(1)}, bf16[5,128,256]{2,1,0:T(8,128)(2,1)}, u32[]{:S(2)}) copy-start(bf16[5,128,256]{2,1,0:T(8,128)(2,1)} %get-tuple-element.112) | copy-start | bytes 983044
  222.2 14.1 %copy-start.8 = (bf16[128,256]{1,0:T(8,128)(2,1)S(1)}, bf16[128,256]{1,0:T(8,128)(2,1)}, u32[]{:S(2)}) copy-start(bf16[128,256]{1,0:T(8,128)(2,1)} %copy-done.7) | copy-start | bytes 196612
  223.0 10.3 %all-to-all-start.2 = ((f32[8,32,256]{2,1,0:T(8,128)}), f32[8,32,256]{2,1,0:T(8,128)S(1)}, u32[]{:S(2)}, u32[]{:S(2)}) async-start(f32[8,32,256]{2,1,0:T(8,128)} %bitcast.41), calls=%async_computation.2 | async-start | bytes 524288 | tf_op jit(solution)/shard_map/all_to_all | solution.py:127
  226.4 96.5 %reduce-scatter.2.cloned.1.call-start = ((), (), s32[]{:S(2)}) async-start(), calls=%async_computation.4 | async-start | bytes 655360 | tf_op jit(solution)/shard_map/reduce_scatter | solution.py:133
Sparse Core Ops, SparseCore 0:
  106.9 68.6 all-reduce.4
  178.0 121.1 all-reduce.6
  302.0 20.8 reduce-scatter.1
